TPU v7x, 256 devices: a whole 4x4x8 slice. The times are simulated.
256 devices in a mesh: dp: 64 (over z_lo, x, y), tensor: 4 (over z_hi, core).
Axes of the slice: x: 4, y: 4, z: 8 (z_hi: 2, z_lo: 4; z = z_hi * 4 + z_lo), core: 2. Of those that a mesh axis runs over, the one named last changes fastest.
Arguments:
- hidden_states: float32 [32768, 2048], P(('dp', 'tensor')), may hold values from -40 to 40
- lengths: int32 [64], P('dp'), may hold values from 128 to 512
- shard_order: int32 [64], replicated, may hold values from 0 to 63, each once
- gain_attn: float32 [2048], replicated, may hold values from 0.25 to 1.75
- w_query: bfloat16 [2048, 2048], P('dp', 'tensor'), may hold values from -0.015625 to 0.015625
- w_key: bfloat16 [2048, 2048], P('dp', 'tensor'), may hold values from -0.125 to 0.125
- w_value: bfloat16 [2048, 2048], P('dp', 'tensor'), may hold values from -0.125 to 0.125
- w_out: bfloat16 [2048, 2048], P('tensor', 'dp'), may hold values from -1 to 1
- rel_bias: float32 [32, 32], P(None, 'tensor'), may hold values from -6 to 300
- gain_ff: float32 [2048], replicated, may hold values from 0.25 to 1.75
- w_gate: bfloat16 [2048, 5120], P('dp', 'tensor'), may hold values from -0.125 to 0.125
- w_up: bfloat16 [2048, 5120], P('dp', 'tensor'), may hold values from -0.125 to 0.125
- w_down: bfloat16 [5120, 2048], P('tensor', 'dp'), may hold values from -0.078125 to 0.078125
- gain_final: float32 [2048], replicated, may hold values from 0.25 to 1.75
- w_reward: float32 [2048], replicated, may hold values from -0.125 to 0.125
Outputs:
- layer_output: float32 [32768, 2048], P(('dp', 'tensor'))
- normalized_rewards: float32 [64], P('dp')
Inputs may be any that keep to these rules, and one draw needn't show every extreme that they name: `shard_order`: each of 0 to 64 - 1 appears once. `lengths`: positions at or beyond a rollout's length are padding.
All inputs are finite; a program needn't handle non-finite values.
Results may differ from a plain program's by a relative error of at most 0.02.
Values may be sent and summed in bfloat16 or wider, within the bound.
A program may use at most 128 MiB of HBM per device.

v0:
```python
import jax
import jax.numpy as jnp
from jax import lax
from jax.sharding import PartitionSpec as P

DK = 64
LEN = 512
bucket_edges = (12, 16, 23, 32, 46, 64, 91)


def in_order(parts, dim):
    parts = jnp.moveaxis(parts, 0, dim)
    shape = parts.shape
    return parts.reshape(*shape[:dim], shape[dim] * shape[dim + 1], *shape[dim + 2 :])


def from_everyone(array, axis):
    peers = lax.axis_size(axis)
    return lax.all_to_all(
        jnp.broadcast_to(array[None], (peers, *array.shape)), axis, 0, 0, tiled=True
    )


def gather_directly(array, axis, dim):
    return in_order(from_everyone(array, axis), dim)


def in_one_piece(arrays, axis, dim, along):
    ends, at = ([], 0)
    for a in arrays[:-1]:
        at += a.shape[along]
        ends.append(at)
    both = jnp.concatenate(arrays, axis=along)
    return tuple(jnp.split(lax.all_gather(both, axis, axis=dim, tiled=True), ends, axis=along))


def cut_along(array, dim, peers):
    shape = array.shape
    parts = array.reshape(*shape[:dim], peers, shape[dim] // peers, *shape[dim + 1 :])
    return jnp.moveaxis(parts, dim, 0)


def sent_and_summed(array, axis, dim):
    peers = lax.axis_size(axis)
    parts = lax.all_to_all(cut_along(array, dim, peers), axis, 0, 0, tiled=True)
    return jnp.sum(parts.astype(jnp.float32), axis=0)


def of_everyone(array, axis):
    return from_everyone(array, axis).sum(axis=0)


def packed_total(arrays, axis):
    line, at, gathered = (jnp.concatenate([a.reshape(-1) for a in arrays]), 0, [])
    running = of_everyone(line, axis)
    for a in arrays:
        gathered.append(running[at : at + a.size].reshape(a.shape))
        at += a.size
    return tuple(gathered)


def bucket_index(relative):
    distance = jnp.abs(relative)
    bucket_low = jnp.minimum(distance, 8)
    for threshold in bucket_edges:
        bucket_low = bucket_low + (distance >= threshold).astype(jnp.int32)
    return jnp.where(relative > 0, 16, 0) + bucket_low


def rms_norm(values_in, weight_gain):
    return (
        values_in
        * lax.rsqrt(jnp.mean(values_in * values_in, axis=-1, keepdims=True) + 1e-06)
        * weight_gain
    )


def reorder_blocks(values_in, ordering):
    full_shape = values_in.shape
    blocks = values_in.reshape(
        full_shape[:-1] + (ordering.shape[0], full_shape[-1] // ordering.shape[0])
    )
    return jnp.take(blocks, ordering, axis=-2).reshape(full_shape)


def local(
    hidden_states,
    lengths,
    shard_order,
    gain_attn,
    w_query,
    w_key,
    w_value,
    w_out,
    rel_bias,
    gain_ff,
    w_gate,
    w_up,
    w_down,
    gain_final,
    w_reward,
):
    groups = shard_order.shape[0]
    block_ids = jnp.arange(groups, dtype=jnp.int32)
    inverse = jnp.sum(
        block_ids[:, None] * (shard_order[:, None] == block_ids[None, :]).astype(jnp.int32), axis=0
    )
    own_rows = reorder_blocks(hidden_states, shard_order)
    attn_gain = reorder_blocks(gain_attn, shard_order)
    feed_gain = reorder_blocks(gain_ff, shard_order)
    final_gain = reorder_blocks(gain_final, shard_order)
    reward_head = reorder_blocks(w_reward, shard_order)
    row_count = own_rows.shape[0]
    row_start = lax.axis_index("tensor") * row_count
    normed = gather_directly(rms_norm(own_rows, attn_gain).astype(jnp.bfloat16), "tensor", 0)

    def contract_with(source):

        def contract(running, portion, offset):
            return jnp.dot(source, portion, preferred_element_type=jnp.float32)

        return contract

    inner_width = w_query.shape[1]
    zero_block = jnp.zeros((LEN, inner_width), jnp.float32)
    attn_contract = contract_with(normed)
    running = (zero_block, zero_block, zero_block)
    portion = in_one_piece((w_query, w_key, w_value), "dp", 0, 1)
    offset = jnp.int32(0)
    queries = attn_contract(running[0], portion[0], offset)
    key_states = attn_contract(running[1], portion[1], offset)
    value_states = attn_contract(running[2], portion[2], offset)
    head_count = inner_width // DK
    query_heads = queries.astype(jnp.bfloat16).reshape(LEN, head_count, DK).transpose(1, 0, 2)
    key_heads = key_states.astype(jnp.bfloat16).reshape(LEN, head_count, DK).transpose(1, 0, 2)
    value_heads = value_states.astype(jnp.bfloat16).reshape(LEN, head_count, DK).transpose(1, 0, 2)
    span = 2 * LEN - 1
    offsets = jnp.arange(span, dtype=jnp.int32)
    relative = jnp.where(offsets < LEN, offsets, offsets - span)
    bucket_ids = bucket_index(relative)
    onehot = (
        bucket_ids[:, None] == jnp.arange(rel_bias.shape[0], dtype=jnp.int32)[None, :]
    ).astype(jnp.float32)
    offset_bias = jnp.dot(onehot, rel_bias, precision=lax.Precision.HIGHEST).T
    length = lengths[0]
    in_range = jnp.arange(LEN, dtype=jnp.int32) < length

    def head_step(operands):
        head_query, head_key, head_value, head_offsets = operands
        repeated = jnp.tile(head_offsets, LEN)[: LEN * (span - 1)].reshape(LEN, span - 1)[:, :LEN]
        scores = jnp.dot(head_query, head_key.T, preferred_element_type=jnp.float32) + repeated
        scores = jnp.where(in_range[None, :], scores, -1e30)
        row_max = jnp.max(scores, axis=-1, keepdims=True)
        exp_scores = jnp.exp(scores - row_max)
        soft_weights = (exp_scores / jnp.sum(exp_scores, axis=-1, keepdims=True)).astype(
            jnp.bfloat16
        )
        return jnp.dot(soft_weights, head_value, preferred_element_type=jnp.float32).astype(
            jnp.bfloat16
        )

    context = lax.map(head_step, (query_heads, key_heads, value_heads, offset_bias))
    context = context.transpose(1, 0, 2).reshape(LEN, inner_width)
    attn_partial = jnp.dot(
        context, lax.all_gather(w_out, "dp", axis=1, tiled=True), preferred_element_type=jnp.float32
    ).astype(jnp.bfloat16)
    mid_own = own_rows + sent_and_summed(attn_partial, "tensor", 0)
    mid_normed = gather_directly(rms_norm(mid_own, feed_gain).astype(jnp.bfloat16), "tensor", 0)
    hidden_width = w_gate.shape[1]
    zero_hidden = jnp.zeros((LEN, hidden_width), jnp.float32)
    feed_contract = contract_with(mid_normed)
    running = (zero_hidden, zero_hidden)
    portion = in_one_piece((w_gate, w_up), "dp", 0, 1)
    offset = jnp.int32(0)
    gate_proj = feed_contract(running[0], portion[0], offset)
    up_proj = feed_contract(running[1], portion[1], offset)
    activated = (jax.nn.gelu(gate_proj, approximate=True) * up_proj).astype(jnp.bfloat16)
    feed_partial = jnp.dot(
        activated,
        lax.all_gather(w_down, "dp", axis=1, tiled=True),
        preferred_element_type=jnp.float32,
    ).astype(jnp.bfloat16)
    output_rows = mid_own + lax.psum_scatter(
        feed_partial, "tensor", scatter_dimension=0, tiled=True
    ).astype(jnp.float32)
    final_normed = rms_norm(output_rows, final_gain)
    token_score = jnp.dot(final_normed, reward_head, precision=lax.Precision.HIGHEST)
    positions = row_start + jnp.arange(row_count, dtype=jnp.int32)
    local_pool = jnp.sum(jnp.where(positions < length, token_score, 0.0))
    pooled_sum = of_everyone(local_pool, "tensor")
    reward = jnp.reshape(pooled_sum / length.astype(jnp.float32), (1,))
    rollouts = lax.axis_size("dp") * lengths.shape[0]
    first_moment, second_moment = packed_total((jnp.sum(reward), jnp.sum(reward * reward)), "dp")
    reward_mean = first_moment / rollouts
    reward_var = second_moment / rollouts - reward_mean * reward_mean
    normalized = (reward - reward_mean) / jnp.sqrt(reward_var + 1e-06)
    return (reorder_blocks(output_rows, inverse), normalized)


def solution(mesh):
    placed = (
        P(("dp", "tensor"), None),
        P("dp"),
        P(),
        P(),
        P("dp", "tensor"),
        P("dp", "tensor"),
        P("dp", "tensor"),
        P("tensor", "dp"),
        P(None, "tensor"),
        P(),
        P("dp", "tensor"),
        P("dp", "tensor"),
        P("tensor", "dp"),
        P(),
        P(),
    )
    return jax.shard_map(
        local,
        mesh=mesh,
        in_specs=placed,
        out_specs=(P(("dp", "tensor"), None), P("dp")),
        check_vma=False,
    )
```

profile of v0, /device:TPU:1, one launch (start us, length us, event | category | flops | bytes accessed | tf_op | source)
XLA Modules:
  0.0 1597.9 jit_solution(13214527331848942773)
XLA Ops:
  7.2 1.5 pad_maximum_fusion.1
  9.6 1.6 pad_maximum_fusion
  19.5 1.7 broadcast_in_dim.58
  21.1 9.9 all-to-all-start
  32.1 48.3 %all-to-all-done = bf16[4,128,2048]{2,1,0:T(8,128)(2,1)S(1)} async-done(((bf16[4,128,2048]{2,1,0:T(8,128)(2,1)}), bf16[4,128,2048]{2,1,0:T(8,128)(2,1)S(1)}, u32[]{:S(2)}, u32[]{:S(2)}) %all-to-all-start) | async-done | bytes 2097184 | tf_op jit(solution)/shard_map/all_to_all | solution.py:19
  80.5 256.9 %all-gather.5.cloned.1.call-done = bf16[2048,1536]{1,0:T(8,128)(2,1)} async-done(((bf16[32,1536]{1,0:T(8,128)(2,1)}), bf16[2048,1536]{1,0:T(8,128)(2,1)}) %all-gather.5.cloned.1.call-update) | async-done | bytes 6291472 | tf_op jit(solution)/shard_map/all_gather | solution.py:34
  337.3 3.7 fusion.39
  341.0 2.4 copy.43
  343.4 3.7 fusion.42
  347.1 2.4 copy.44
  349.5 3.7 fusion.45
  353.2 2.4 copy.45
  355.7 103.8 %while.11 = (s32[]{:T(128)}, bf16[8,512,64]{1,2,0:T(8,128)(2,1)}, bf16[8,512,64]{2,1,0:T(8,128)(2,1)}, bf16[8,512,64]{2,1,0:T(8,128)(2,1)}, f32[8,1023]{1,0:T(8,...) while((s32[]{:T(128)}, bf16[8,512,64]{1,2,0:T(8,128)(2,1)}, ...), condition=%wide.region_4.7_spmd.clone, body=%wide.region_1.6_spmd.clone.sunk | while | flops 69238272 | bytes 26672264 | solution.py:162
  355.9 2.7 tile.17
  358.6 1.6 slice-done
  360.2 2.9 reshape.327
  366.8 1.9 fusion.90
  368.9 2.7 tile.17
  371.6 1.6 slice-done
  373.2 2.9 reshape.327
  379.8 1.8 fusion.90
  381.9 2.7 tile.17
  384.6 1.6 slice-done
  386.2 2.9 reshape.327
  392.8 1.8 fusion.90
  394.9 2.7 tile.17
  397.5 1.6 slice-done
  399.1 2.9 reshape.327
  404.2 1.3 fusion.88
  405.7 1.8 fusion.90
  407.8 2.7 tile.17
  410.5 1.6 slice-done
  412.1 2.9 reshape.327
  418.7 1.8 fusion.90
  420.8 2.7 tile.17
  423.5 1.6 slice-done
  425.1 2.9 reshape.327
  431.7 1.8 fusion.90
  433.8 2.7 tile.17
  436.5 1.6 slice-done
  438.1 2.9 reshape.327
  444.7 1.8 fusion.90
  446.8 2.7 tile.17
  449.4 1.6 slice-done
  451.0 2.9 reshape.327
  457.6 1.8 fusion.90
  459.5 227.3 %all-gather.7.cloned.1.call-done = bf16[512,2048]{0,1:T(8,128)(2,1)} async-done(((bf16[512,32]{0,1:T(8,128)(2,1)}), bf16[512,2048]{0,1:T(8,128)(2,1)}) %all-gather.7.cloned.1.call-update) | async-done | bytes 2097168 | tf_op jit(solution)/shard_map/all_gather | solution.py:165
  686.8 4.4 convolution_convert_fusion.2
  691.2 86.6 %all-to-all-start.1 = ((bf16[4,128,2048]{2,1,0:T(8,128)(2,1)}), bf16[4,128,2048]{2,1,0:T(8,128)(2,1)}, u32[]{:S(2)}, u32[]{:S(2)}) async-start(bf16[4,128,2048]{2,1,0:T(8,128)(2,1)} %bitcast.15), calls=%async_computation.1 | async-start | bytes 4194304 | tf_op jit(solution)/shard_map/all_to_all | solution.py:45
  778.0 1.3 copy.46
  779.3 36.6 %all-to-all-done.1 = bf16[4,128,2048]{2,1,0:T(8,128)(2,1)} async-done(((bf16[4,128,2048]{2,1,0:T(8,128)(2,1)}), bf16[4,128,2048]{2,1,0:T(8,128)(2,1)}, u32[]{:S(2)}, u32[]{:S(2)}) %all-to-all-start.1) | async-done | bytes 2097184 | tf_op jit(solution)/shard_map/all_to_all | solution.py:45
  815.9 2.1 convert_reduce_fusion
  820.1 44.2 %all_to_all.27 = bf16[4,128,2048]{2,1,0:T(8,128)(2,1)} all-to-all(bf16[4,128,2048]{2,1,0:T(8,128)(2,1)S(1)} %broadcast_in_dim.85), channel_id=1, replica_groups=mesh['dp'=64,'tensor'=4] {'tensor'}, dimensions={0} | all-to-all | bytes 4194304 | tf_op jit(solution)/shard_map/all_to_all | solution.py:19
  864.3 226.2 %all-gather.9.cloned.1.call-done = bf16[2048,2560]{1,0:T(8,128)(2,1)} async-done(((bf16[32,2560]{1,0:T(8,128)(2,1)}), bf16[2048,2560]{1,0:T(8,128)(2,1)}) %all-gather.9.cloned.1.call-update) | async-done | bytes 10485776 | tf_op jit(solution)/shard_map/all_gather | solution.py:34
  1090.5 7.8 fusion.30
  1098.3 341.8 %all-gather.11.cloned.1.call-done = bf16[1280,2048]{0,1:T(8,128)(2,1)} async-done(((bf16[1280,32]{0,1:T(8,128)(2,1)}), bf16[1280,2048]{0,1:T(8,128)(2,1)}) %all-gather.11.cloned.1.call-update) | async-done | bytes 5242896 | tf_op jit(solution)/shard_map/all_gather | solution.py:180
  1440.1 13.1 convolution_convert_fusion.1
  1454.2 98.7 %reduce-scatter.2.cloned.1.call-done = bf16[128,2048]{1,0:T(8,128)(2,1)} async-done(((bf16[512,2048]{1,0:T(8,128)(2,1)}), bf16[128,2048]{1,0:T(8,128)(2,1)}) %reduce-scatter.2.cloned.1.call-update) | async-done | bytes 524304 | tf_op jit(solution)/shard_map/reduce_scatter | solution.py:183
  1554.5 1.7 fusion.56
  1557.5 4.0 all-to-all-start.3
  1562.2 6.3 all-to-all-done.3
  1570.4 7.6 all-to-all-start.4
  1578.2 1.3 copy.51
  1579.5 7.6 all-to-all-done.4
  (136 shorter events, 48.4 us)
Async XLA Ops:
  7.2 24.5 %copy-start = (f32[32,8]{0,1:T(8,128)S(1)}, f32[32,8]{0,1:T(8,128)}, u32[]{:S(2)}) copy-start(f32[32,8]{0,1:T(8,128)} %param.29) | copy-start | bytes 3076
  7.2 10.2 copy-start.3
  7.2 330.1 %all-gather.5.cloned.1.call-start = ((), (), s32[]{:S(2)}) async-start(), calls=%async_computation.6 | async-start | bytes 6389760 | tf_op jit(solution)/shard_map/all_gather | solution.py:34
  8.8 678.1 %all-gather.7.cloned.1.call-start = ((), (), s32[]{:S(2)}) async-start(), calls=%async_computation.7 | async-start | bytes 2129920 | tf_op jit(solution)/shard_map/all_gather | solution.py:165
  9.5 1080.9 %all-gather.9.cloned.1.call-start = ((), (), s32[]{:S(2)}) async-start(), calls=%async_computation.8 | async-start | bytes 10649600 | tf_op jit(solution)/shard_map/all_gather | solution.py:34
  17.7 0.7 copy-start.4
  21.1 59.3 %all-to-all-start = ((bf16[4,128,2048]{2,1,0:T(8,128)(2,1)}), bf16[4,128,2048]{2,1,0:T(8,128)(2,1)S(1)}, u32[]{:S(2)}, u32[]{:S(2)}) async-start(bf16[4,128,2048]{2,1,0:T(8,128)(2,1)} %broadcast_in_dim.58), calls=%async_computation | async-start | bytes 4194304 | tf_op jit(solution)/shard_map/all_to_all | solution.py:19
  31.1 1409.0 %all-gather.11.cloned.1.call-start = ((), (), s32[]{:S(2)}) async-start(), calls=%async_computation.9 | async-start | bytes 5324800 | tf_op jit(solution)/shard_map/all_gather | solution.py:180
  358.6 1.6 slice-start
  363.1 1.2 slice-start.1
  371.6 1.6 slice-start
  376.1 1.2 slice-start.1
  384.6 1.6 slice-start
  389.1 1.2 slice-start.1
  397.5 1.6 slice-start
  402.0 1.2 slice-start.1
  410.5 1.6 slice-start
  415.0 1.2 slice-start.1
  423.5 1.6 slice-start
  428.0 1.2 slice-start.1
  436.5 1.6 slice-start
  441.0 1.2 slice-start.1
  449.4 1.6 slice-start
  453.9 1.2 slice-start.1
  691.2 124.7 %all-to-all-start.1 = ((bf16[4,128,2048]{2,1,0:T(8,128)(2,1)}), bf16[4,128,2048]{2,1,0:T(8,128)(2,1)}, u32[]{:S(2)}, u32[]{:S(2)}) async-start(bf16[4,128,2048]{2,1,0:T(8,128)(2,1)} %bitcast.15), calls=%async_computation.1 | async-start | bytes 4194304 | tf_op jit(solution)/shard_map/all_to_all | solution.py:45
  777.9 775.0 %reduce-scatter.2.cloned.1.call-start = ((), (), s32[]{:S(2)}) async-start(), calls=%async_computation.10 | async-start | bytes 2621440 | tf_op jit(solution)/shard_map/reduce_scatter | solution.py:183
  818.3 1.2 copy-start.2
  1557.5 11.0 all-to-all-start.3
  1561.5 28.7 %copy-start.1 = (f32[32,8]{0,1:T(8,128)S(1)}, f32[32,8]{0,1:T(8,128)}, u32[]{:S(2)}) copy-start(f32[32,8]{0,1:T(8,128)} %param.29) | copy-start | bytes 3076
  1570.4 16.7 %all-to-all-start.4 = ((f32[64,1,2]{2,1,0:T(1,128)}), f32[64,1,2]{2,1,0:T(1,128)S(1)}, u32[]{:S(2)}, u32[]{:S(2)}) async-start(f32[64,1,2]{2,1,0:T(1,128)} %broadcast_in_dim.88), calls=%async_computation.5 | async-start | bytes 65536 | tf_op jit(solution)/shard_map/all_to_all | solution.py:19
Sparse Core Ops, SparseCore 0:
  10.4 326.9 all-gather.4
  339.1 347.6 all-gather.6
  688.6 401.8 all-gather.8
  1092.1 347.8 all-gather.10
  1453.3 99.5 reduce-scatter.1
where the time goes:
time: 1600 us
  waiting for transfers between devices  1250 us (78%)
  starting transfers between devices  108 us (7%)
  local copies, waits for them, and re-layouts  95.1 us (6%)
  matrix products  63.7 us (4%)
  blocking collectives  44.2 us (3%)
  between operations  18.8 us (1%)
  other arithmetic  16.4 us (1%)
    all_gather x2, waiting for transfers between devices, in_one_piece(): lax.all_gather(both, axis, axis=dim, tiled=True)  483 us
    all_gather x1, waiting for transfers between devices, local(): lax.all_gather(w_down, 'dp', axis=1, tiled=True)  342 us
    all_gather x1, waiting for transfers between devices, local(): lax.all_gather(w_out, 'dp', axis=1, tiled=True)  227 us
    reduce_scatter x1, waiting for transfers between devices, local(): lax.psum_scatter(feed_partial, 'tensor', scatter_dimension=0, tiled=True)  98.7 us
    all_to_all x1, starting transfers between devices, sent_and_summed(): parts = lax.all_to_all(cut_along(array, dim, peers), axis, 0, 0, tiled=True)  86.6 us
    all_to_all x3, waiting for transfers between devices, from_everyone(): lax.all_to_all(jnp.broadcast_to(array[None], (peers, *array.shape)), axis...  62.2 us
    all_to_all x1, blocking collectives, from_everyone(): lax.all_to_all(jnp.broadcast_to(array[None], (peers, *array.shape)), axis...  44.2 us
    all_to_all x1, waiting for transfers between devices, sent_and_summed(): parts = lax.all_to_all(cut_along(array, dim, peers), axis, 0, 0, tiled=True)  36.6 us
  transfers between devices with their start and end apart: 9, of which 9 were waited for; matrix products, arithmetic and copies ran while one was open for 8% of the time, Pallas kernels for 0%

commit v1 on v0

--- a/solution.py
+++ b/solution.py
@@ -6,6 +6,11 @@
 DK = 64
 LEN = 512
 bucket_edges = (12, 16, 23, 32, 46, 64, 91)
+
+
+def exchange_gather(block, mesh_axis, dim):
+    repeated = jnp.stack([block] * lax.axis_size(mesh_axis))
+    return jnp.concatenate(lax.all_to_all(repeated, mesh_axis, 0, 0), axis=dim)
 
 
 def in_order(parts, dim):
@@ -162,7 +167,7 @@
     context = lax.map(head_step, (query_heads, key_heads, value_heads, offset_bias))
     context = context.transpose(1, 0, 2).reshape(LEN, inner_width)
     attn_partial = jnp.dot(
-        context, lax.all_gather(w_out, "dp", axis=1, tiled=True), preferred_element_type=jnp.float32
+        context, exchange_gather(w_out, "dp", 1), preferred_element_type=jnp.float32
     ).astype(jnp.bfloat16)
     mid_own = own_rows + sent_and_summed(attn_partial, "tensor", 0)
     mid_normed = gather_directly(rms_norm(mid_own, feed_gain).astype(jnp.bfloat16), "tensor", 0)

time: 1600 us -> 1270 us (0.79)
  waiting for transfers between devices: 1250 us -> 926 us
    all_gather x1 -> x0, waiting for transfers between devices: 227 us -> none  [local(): lax.all_gather(w_out, 'dp', axis=1, tiled=True)]
    all_gather x2, waiting for transfers between devices: 483 us -> 373 us  [in_one_piece(): lax.all_gather(both, axis, axis=dim, tiled=True)]
    all_to_all x1, starting transfers between devices: 86.6 us -> 53.6 us  [sent_and_summed(): parts = lax.all_to_all(cut_along(array, dim, peers), axis, 0, 0, tiled=True)]
    all_to_all x0 -> x1, starting transfers between devices: none -> 22.7 us  [exchange_gather(): return jnp.concatenate(lax.all_to_all(repeated, mesh_axis, 0, 0), axis=dim)]
  transfers between devices with their start and end apart: 9 -> 9, of which waited for: 9 -> 8; matrix products, arithmetic and copies ran while one was open for 8% -> 10% of each run, Pallas kernels for 0% -> 0%
where the time goes in v1:
time: 1270 us
  waiting for transfers between devices  926 us (73%)
  starting transfers between devices  98.2 us (8%)
  local copies, waits for them, and re-layouts  96.7 us (8%)
  matrix products  63.7 us (5%)
  blocking collectives  45.5 us (4%)
  between operations  18.8 us (1%)
  other arithmetic  16.4 us (1%)
    all_gather x2, waiting for transfers between devices, in_one_piece(): lax.all_gather(both, axis, axis=dim, tiled=True)  373 us
    all_gather x1, waiting for transfers between devices, local(): lax.all_gather(w_down, 'dp', axis=1, tiled=True)  343 us
    reduce_scatter x1, waiting for transfers between devices, local(): lax.psum_scatter(feed_partial, 'tensor', scatter_dimension=0, tiled=True)  98.7 us
    all_to_all x3, waiting for transfers between devices, from_everyone(): lax.all_to_all(jnp.broadcast_to(array[None], (peers, *array.shape)), axis...  59.2 us
    all_to_all x1, starting transfers between devices, sent_and_summed(): parts = lax.all_to_all(cut_along(array, dim, peers), axis, 0, 0, tiled=True)  53.6 us
    all_to_all x1, waiting for transfers between devices, sent_and_summed(): parts = lax.all_to_all(cut_along(array, dim, peers), axis, 0, 0, tiled=True)  51.9 us
    all_to_all x1, blocking collectives, from_everyone(): lax.all_to_all(jnp.broadcast_to(array[None], (peers, *array.shape)), axis...  45.5 us
  transfers between devices with their start and end apart: 9, of which 8 were waited for; matrix products, arithmetic and copies ran while one was open for 10% of the time, Pallas kernels for 0%

profile of v1, /device:TPU:1, one launch (start us, length us, event | category | flops | bytes accessed | tf_op | source)
XLA Modules:
  0.0 1265.9 jit_solution(7353563323077735729)
XLA Ops:
  7.2 1.5 pad_maximum_fusion.1
  8.8 1.6 pad_maximum_fusion
  18.7 1.6 broadcast_in_dim.58
  20.4 10.1 all-to-all-start
  31.6 45.4 %all-to-all-done = bf16[4,128,2048]{2,1,0:T(8,128)(2,1)S(1)} async-done(((bf16[4,128,2048]{2,1,0:T(8,128)(2,1)}), bf16[4,128,2048]{2,1,0:T(8,128)(2,1)S(1)}, u32[]{:S(2)}, u32[]{:S(2)}) %all-to-all-start) | async-done | bytes 2097184 | tf_op jit(solution)/shard_map/all_to_all | solution.py:24
  77.0 1.6 stack.2
  78.6 22.7 %all-to-all-start.1 = ((bf16[64,512,32]{1,2,0:T(8,128)(2,1)}), bf16[64,512,32]{1,2,0:T(8,128)(2,1)}, u32[]{:S(2)}, u32[]{:S(2)}) async-start(bf16[64,512,32]{1,2,0:T(8,128)(2,1)} %stack.2), calls=%async_computation.1 | async-start | bytes 4194304 | tf_op jit(solution)/shard_map/all_to_all | solution.py:13
  101.4 245.4 %all-gather.4.cloned.1.call-done = bf16[2048,1536]{1,0:T(8,128)(2,1)} async-done(((bf16[32,1536]{1,0:T(8,128)(2,1)}), bf16[2048,1536]{1,0:T(8,128)(2,1)}) %all-gather.4.cloned.1.call-update) | async-done | bytes 6291472 | tf_op jit(solution)/shard_map/all_gather | solution.py:39
  346.8 3.7 fusion.39
  350.5 2.4 copy.44
  352.9 3.7 fusion.42
  356.6 2.3 copy.45
  358.9 3.7 fusion.45
  362.6 2.4 copy.46
  365.1 103.9 %while.11 = (s32[]{:T(128)}, bf16[8,512,64]{1,2,0:T(8,128)(2,1)}, bf16[8,512,64]{2,1,0:T(8,128)(2,1)}, bf16[8,512,64]{2,1,0:T(8,128)(2,1)}, f32[8,1023]{1,0:T(8,...) while((s32[]{:T(128)}, bf16[8,512,64]{1,2,0:T(8,128)(2,1)}, ...), condition=%wide.region_4.7_spmd.clone, body=%wide.region_1.6_spmd.clone.sunk | while | flops 69238272 | bytes 26672264 | solution.py:167
  365.3 2.7 tile.17
  368.0 1.6 slice-done
  369.6 2.9 reshape.337
  376.2 1.8 fusion.90
  378.3 2.7 tile.17
  381.0 1.6 slice-done
  382.6 2.9 reshape.337
  389.2 1.8 fusion.90
  391.3 2.7 tile.17
  393.9 1.6 slice-done
  395.5 2.9 reshape.337
  402.1 1.8 fusion.90
  404.3 2.7 tile.17
  406.9 1.6 slice-done
  408.5 2.9 reshape.337
  415.1 1.8 fusion.90
  417.2 2.7 tile.17
  419.9 1.6 slice-done
  421.5 2.9 reshape.337
  428.1 1.8 fusion.90
  430.2 2.7 tile.17
  432.9 1.6 slice-done
  434.5 2.9 reshape.337
  441.1 1.8 fusion.90
  443.2 2.7 tile.17
  445.9 1.6 slice-done
  447.5 2.9 reshape.337
  454.1 1.8 fusion.90
  456.2 2.7 tile.17
  458.9 1.6 slice-done
  460.5 2.9 reshape.337
  467.1 1.8 fusion.90
  468.9 4.4 convolution_convert_fusion.2
  473.4 53.6 %all-to-all-start.2 = ((bf16[4,128,2048]{2,1,0:T(8,128)(2,1)}), bf16[4,128,2048]{2,1,0:T(8,128)(2,1)}, u32[]{:S(2)}, u32[]{:S(2)}) async-start(bf16[4,128,2048]{2,1,0:T(8,128)(2,1)} %bitcast.17), calls=%async_computation.2 | async-start | bytes 4194304 | tf_op jit(solution)/shard_map/all_to_all | solution.py:50
  527.1 1.3 copy.47
  528.4 51.9 %all-to-all-done.2 = bf16[4,128,2048]{2,1,0:T(8,128)(2,1)} async-done(((bf16[4,128,2048]{2,1,0:T(8,128)(2,1)}), bf16[4,128,2048]{2,1,0:T(8,128)(2,1)}, u32[]{:S(2)}, u32[]{:S(2)}) %all-to-all-start.2) | async-done | bytes 2097184 | tf_op jit(solution)/shard_map/all_to_all | solution.py:50
  580.2 2.1 convert_reduce_fusion
  584.4 45.5 %all_to_all.32 = bf16[4,128,2048]{2,1,0:T(8,128)(2,1)} all-to-all(bf16[4,128,2048]{2,1,0:T(8,128)(2,1)S(1)} %broadcast_in_dim.85), channel_id=1, replica_groups=mesh['dp'=64,'tensor'=4] {'tensor'}, dimensions={0} | all-to-all | bytes 4194304 | tf_op jit(solution)/shard_map/all_to_all | solution.py:24
  629.8 127.9 %all-gather.6.cloned.1.call-done = bf16[2048,2560]{1,0:T(8,128)(2,1)} async-done(((bf16[32,2560]{1,0:T(8,128)(2,1)}), bf16[2048,2560]{1,0:T(8,128)(2,1)}) %all-gather.6.cloned.1.call-update) | async-done | bytes 10485776 | tf_op jit(solution)/shard_map/all_gather | solution.py:39
  757.7 7.8 fusion.30
  765.6 342.5 %all-gather.8.cloned.1.call-done = bf16[1280,2048]{0,1:T(8,128)(2,1)} async-done(((bf16[1280,32]{0,1:T(8,128)(2,1)}), bf16[1280,2048]{0,1:T(8,128)(2,1)}) %all-gather.8.cloned.1.call-update) | async-done | bytes 5242896 | tf_op jit(solution)/shard_map/all_gather | solution.py:185
  1108.1 13.1 %convolution_convert_fusion.1 = bf16[512,2048]{1,0:T(8,128)(2,1)} fusion(bf16[1280,2048]{0,1:T(8,128)(2,1)} %all-gather.8.cloned.1.call-done, f32[512,1280]{1,0:T(8,128)} %fusion.30, bf16[512,2048]{1,0:T(8,128)(2,1)} %bitcast.94, bf16[2048,2560]{1,0:T(8,128)(2,1)} %all-gather.6.cloned.1.call-done), kind=kOutput, calls=%fused_computation.33 | convolution fusion | flops 5371068416 | bytes 17301504 | tf_op jit(solution)/shard_map/dot_general | solution.py:183
  1122.2 98.7 %reduce-scatter.2.cloned.1.call-done = bf16[128,2048]{1,0:T(8,128)(2,1)} async-done(((bf16[512,2048]{1,0:T(8,128)(2,1)}), bf16[128,2048]{1,0:T(8,128)(2,1)}) %reduce-scatter.2.cloned.1.call-update) | async-done | bytes 524304 | tf_op jit(solution)/shard_map/reduce_scatter | solution.py:188
  1222.5 1.7 fusion.56
  1225.5 4.0 all-to-all-start.4
  1230.2 6.3 all-to-all-done.4
  1238.4 7.6 all-to-all-start.5
  1246.2 1.3 copy.52
  1247.5 7.6 all-to-all-done.5
  (138 shorter events, 49.2 us)
Async XLA Ops:
  7.2 24.0 %copy-start = (f32[32,8]{0,1:T(8,128)S(1)}, f32[32,8]{0,1:T(8,128)}, u32[]{:S(2)}) copy-start(f32[32,8]{0,1:T(8,128)} %param.29) | copy-start | bytes 3076
  7.2 9.4 copy-start.3
  7.2 339.6 %all-gather.4.cloned.1.call-start = ((), (), s32[]{:S(2)}) async-start(), calls=%async_computation.7 | async-start | bytes 6389760 | tf_op jit(solution)/shard_map/all_gather | solution.py:39
  8.8 749.0 %all-gather.6.cloned.1.call-start = ((), (), s32[]{:S(2)}) async-start(), calls=%async_computation.8 | async-start | bytes 10649600 | tf_op jit(solution)/shard_map/all_gather | solution.py:39
  16.9 0.7 copy-start.5
  20.3 56.7 %copy-start.4 = (bf16[512,32]{0,1:T(8,128)(2,1)S(1)}, bf16[512,32]{0,1:T(8,128)(2,1)}, u32[]{:S(2)}) copy-start(bf16[512,32]{0,1:T(8,128)(2,1)} %param.28) | copy-start | bytes 98308
  20.4 56.7 %all-to-all-start = ((bf16[4,128,2048]{2,1,0:T(8,128)(2,1)}), bf16[4,128,2048]{2,1,0:T(8,128)(2,1)S(1)}, u32[]{:S(2)}, u32[]{:S(2)}) async-start(bf16[4,128,2048]{2,1,0:T(8,128)(2,1)} %broadcast_in_dim.58), calls=%async_computation | async-start | bytes 4194304 | tf_op jit(solution)/shard_map/all_to_all | solution.py:24
  30.4 1077.7 %all-gather.8.cloned.1.call-start = ((), (), s32[]{:S(2)}) async-start(), calls=%async_computation.9 | async-start | bytes 5324800 | tf_op jit(solution)/shard_map/all_gather | solution.py:185
  78.6 390.3 %all-to-all-start.1 = ((bf16[64,512,32]{1,2,0:T(8,128)(2,1)}), bf16[64,512,32]{1,2,0:T(8,128)(2,1)}, u32[]{:S(2)}, u32[]{:S(2)}) async-start(bf16[64,512,32]{1,2,0:T(8,128)(2,1)} %stack.2), calls=%async_computation.1 | async-start | bytes 4194304 | tf_op jit(solution)/shard_map/all_to_all | solution.py:13
  368.0 1.6 slice-start
  372.5 1.2 slice-start.1
  381.0 1.6 slice-start
  385.5 1.2 slice-start.1
  393.9 1.6 slice-start
  398.4 1.2 slice-start.1
  406.9 1.6 slice-start
  411.4 1.2 slice-start.1
  419.9 1.6 slice-start
  424.4 1.2 slice-start.1
  432.9 1.6 slice-start
  437.4 1.2 slice-start.1
  445.9 1.6 slice-start
  450.4 1.2 slice-start.1
  458.9 1.6 slice-start
  463.4 1.2 slice-start.1
  473.4 106.9 %all-to-all-start.2 = ((bf16[4,128,2048]{2,1,0:T(8,128)(2,1)}), bf16[4,128,2048]{2,1,0:T(8,128)(2,1)}, u32[]{:S(2)}, u32[]{:S(2)}) async-start(bf16[4,128,2048]{2,1,0:T(8,128)(2,1)} %bitcast.17), calls=%async_computation.2 | async-start | bytes 4194304 | tf_op jit(solution)/shard_map/all_to_all | solution.py:50
  527.0 693.9 %reduce-scatter.2.cloned.1.call-start = ((), (), s32[]{:S(2)}) async-start(), calls=%async_computation.10 | async-start | bytes 2621440 | tf_op jit(solution)/shard_map/reduce_scatter | solution.py:188
  582.7 1.2 copy-start.2
  1225.5 11.0 all-to-all-start.4
  1229.5 28.7 %copy-start.1 = (f32[32,8]{0,1:T(8,128)S(1)}, f32[32,8]{0,1:T(8,128)}, u32[]{:S(2)}) copy-start(f32[32,8]{0,1:T(8,128)} %param.29) | copy-start | bytes 3076
  1238.4 16.7 %all-to-all-start.5 = ((f32[64,1,2]{2,1,0:T(1,128)}), f32[64,1,2]{2,1,0:T(1,128)S(1)}, u32[]{:S(2)}, u32[]{:S(2)}) async-start(f32[64,1,2]{2,1,0:T(1,128)} %broadcast_in_dim.88), calls=%async_computation.6 | async-start | bytes 65536 | tf_op jit(solution)/shard_map/all_to_all | solution.py:24
Sparse Core Ops, SparseCore 0:
  10.4 336.4 all-gather.3
  348.6 409.0 all-gather.5
  759.5 348.4 all-gather.7
  1121.4 99.5 reduce-scatter.1
